TPU v7x, 32 devices: a whole 2x2x4 slice. The times are simulated.
32 devices in a mesh: groups: 2 (over x), tm: 4 (over y, core), rows: 4 (over z).
Axes of the slice: x: 2, y: 2, z: 4, core: 2. Of those that a mesh axis runs over, the one named last changes fastest.
Arguments:
- features: bfloat16 [16, 8, 96, 512], P(('groups', 'tm'), 'rows'), parts along dimension 0, may hold values from -6 to 6
- spatial_weight: bfloat16 [3, 3, 512, 512], replicated, may hold values from -0.09375 to 0.09375
- temporal_weight: bfloat16 [3, 512, 512], replicated, may hold values from -0.15625 to 0.15625
- head_weight: bfloat16 [512, 16], replicated, may hold values from -0.25 to 0.25
- embed_weight: bfloat16 [64, 5120], replicated, may hold values from -0.75 to 0.75
- ada_scale: bfloat16 [5120], replicated, may hold values from -0.5 to 0.5
- ada_shift: bfloat16 [5120], replicated, may hold values from -3 to 3
- qkv_weight: bfloat16 [5120, 9216], P('tm', 'rows'), may hold values from -0.078125 to 0.078125
Outputs:
- qkv: float32 [3072, 9216], P(('groups', 'tm'), 'rows'), parts along dimension 0
There are 2 independent parts, one for each index of `groups`. A program takes and returns all parts, laid end to end along the dimension named above; an argument that names none is the same for every part. Nothing has to cross between parts.
All inputs are finite; a program needn't handle non-finite values.
Results may differ from a plain program's by a relative error of at most 0.0056.
Values may be sent and summed in bfloat16 or wider, within the bound.
A program may use at most 128 MiB of HBM per device.

v0:
```python
import jax
import jax.numpy as jnp
from jax import lax
from jax.sharding import PartitionSpec as P

LATENT = 16
PATCH = 2
PDIM = 64


def with_halo(cells, sides, width):
    for axis, dim in sides:
        count = lax.axis_size(axis)
        ends = count - 1
        head = lax.slice_in_dim(cells, 0, width, axis=dim)
        tail = lax.slice_in_dim(cells, cells.shape[dim] - width, cells.shape[dim], axis=dim)
        cells = jnp.concatenate(
            [
                lax.ppermute(tail, axis, [(i, (i + 1) % count) for i in range(ends)]),
                cells,
                lax.ppermute(head, axis, [((i + 1) % count, i) for i in range(ends)]),
            ],
            axis=dim,
        )
    return cells


def passed_along(block, axis, distance):
    devices = range(lax.axis_size(axis))
    route = [(i - distance, i) for i in devices if i - distance in devices]
    return lax.ppermute(block, axis, route)


def norm_silu(values):
    scaled = values * lax.rsqrt(jnp.mean(values * values, axis=-1, keepdims=True) + 1e-06)
    return jax.nn.silu(scaled)


def per_device(
    features,
    spatial_weight,
    temporal_weight,
    head_weight,
    embed_weight,
    ada_scale,
    ada_shift,
    qkv_weight,
):
    frames_dev, rows_dev, columns, channels = features.shape
    activated = norm_silu(features.astype(jnp.float32)).astype(jnp.bfloat16)
    rimmed = with_halo(activated, (("rows", 1),), 1)
    padded = jnp.pad(rimmed, ((0, 0), (0, 0), (1, 1), (0, 0)))
    spatial = jnp.zeros((frames_dev * rows_dev * columns, channels), jnp.float32)
    for tap_row in range(3):
        for tap_col in range(3):
            window = padded[:, tap_row : tap_row + rows_dev, tap_col : tap_col + columns].reshape(
                -1, channels
            )
            spatial = spatial + jnp.dot(
                window, spatial_weight[tap_row, tap_col], preferred_element_type=jnp.float32
            )
    mixed_act = (
        norm_silu(spatial).astype(jnp.bfloat16).reshape(frames_dev, rows_dev, columns, channels)
    )
    before = passed_along(mixed_act, "tm", 1)
    stacked = jnp.concatenate([before, mixed_act], axis=0)
    temporal = jnp.zeros((frames_dev * rows_dev * columns, channels), jnp.float32)
    for tap in range(3):
        temporal = temporal + jnp.dot(
            stacked[tap : tap + frames_dev].reshape(-1, channels),
            temporal_weight[tap],
            preferred_element_type=jnp.float32,
        )
    summed = features.astype(jnp.float32).reshape(-1, channels) + temporal
    latent = jnp.dot(
        norm_silu(summed).astype(jnp.bfloat16), head_weight, preferred_element_type=jnp.float32
    ).astype(jnp.bfloat16)
    latent = latent.reshape(frames_dev, 1, PATCH, columns // PATCH, PATCH, LATENT)
    patches = jnp.transpose(latent, (0, 1, 3, 2, 4, 5)).reshape(
        frames_dev, 1, columns // PATCH, PDIM
    )
    token_block = lax.all_gather(patches, "rows", axis=1, tiled=True)
    block_rows = token_block.shape[0] * token_block.shape[1] * token_block.shape[2]
    embedded = jnp.dot(
        token_block.reshape(block_rows, PDIM), embed_weight, preferred_element_type=jnp.float32
    ).astype(jnp.bfloat16)
    widened = lax.optimization_barrier(embedded).astype(jnp.float32)
    centered = widened - jnp.mean(widened, axis=-1, keepdims=True)
    spread = jnp.mean(centered * centered, axis=-1, keepdims=True)
    modulated = centered * lax.rsqrt(spread + 1e-06) * (
        1.0 + ada_scale.astype(jnp.float32)
    ) + ada_shift.astype(jnp.float32)
    normalized = modulated.astype(jnp.bfloat16)
    whole_columns = lax.all_gather(qkv_weight, "tm", axis=0, tiled=True)
    projected = jnp.dot(normalized, whole_columns, preferred_element_type=jnp.float32)
    return projected


def solution(mesh):
    return jax.shard_map(
        per_device,
        mesh=mesh,
        in_specs=(
            P(("groups", "tm"), "rows", None, None),
            P(),
            P(),
            P(),
            P(),
            P(),
            P(),
            P("tm", "rows"),
        ),
        out_specs=P(("groups", "tm"), "rows"),
        check_vma=False,
    )
```

profile of v0, /device:TPU:7, one launch (start us, length us, event | category | flops | bytes accessed | tf_op | source)
XLA Modules:
  0.0 185.0 jit_solution(10699574002116954827)
XLA Ops:
  6.5 0.0 copy-start
  6.5 0.0 copy-start.2
  6.5 0.0 copy-start.4
  6.5 0.0 all-gather.2.cloned.1.call-start
  6.5 0.0 slice-start
  6.6 0.7 all-gather.2.cloned.1.call-update
  7.3 0.3 copy-done.2
  7.6 0.2 multiply_reduce_fusion.2
  7.8 0.3 multiply_convert_fusion.2
  8.1 3.2 %collective-permute-start = (bf16[2,1,96,512]{3,2,1,0:T(8,128)(2,1)S(1)}, bf16[2,1,96,512]{3,2,1,0:T(8,128)(2,1)S(1)}, u32[]{:S(2)}, u32[]{:S(2)}) collective-permute-start(bf16[2,1,96,512]{3,2,1,0:T(8,128)(2,1)S(1)} %get-tuple-element.13), channel_id=1, source_target_pairs={{0,1},{1,2},{2,3},{4,5},{5,6},{6,7},{8,9},{9,10},{10,11},{12,13},{... | collective-permute-start | bytes 589832 | tf_op jit(solution)/shard_map/ppermute | solution.py:19
  11.3 1.3 collective-permute-start.1
  12.6 0.0 copy-done.4
  12.7 0.0 slice-start.1
  12.7 2.2 %collective-permute-done = bf16[2,1,96,512]{3,2,1,0:T(8,128)(2,1)S(1)} collective-permute-done((bf16[2,1,96,512]{3,2,1,0:T(8,128)(2,1)S(1)}, bf16[2,1,96,512]{3,2,1,0:T(8,128)(2,1)S(1)}, u32[]{:S(2)}, u32[]{:S(2)}) %collective-permute-start) | collective-permute-done | bytes 196640 | tf_op jit(solution)/shard_map/ppermute | solution.py:19
  14.9 3.8 %collective-permute-done.1 = bf16[2,1,96,512]{3,2,1,0:T(8,128)(2,1)S(1)} collective-permute-done((bf16[2,1,96,512]{3,2,1,0:T(8,128)(2,1)S(1)}, bf16[2,1,96,512]{3,2,1,0:T(8,128)(2,1)S(1)}, u32[]{:S(2)}, u32[]{:S(2)}) %collective-permute-start.1) | collective-permute-done | bytes 196640 | tf_op jit(solution)/shard_map/ppermute | solution.py:21
  18.7 0.1 pad_maximum_fusion.1
  18.8 0.2 fusion.20
  19.0 0.3 fusion.50
  19.4 0.0 slice-done
  19.4 0.0 slice-done.1
  19.4 0.4 fusion.35
  19.8 0.4 fusion.26
  20.1 0.4 convolution_add_fusion.7
  20.5 0.4 convolution_add_fusion.6
  20.9 0.4 convolution_add_fusion.5
  21.3 0.4 convolution_add_fusion.4
  21.6 0.0 copy-start.5
  21.6 0.0 copy-start.3
  21.7 0.4 convolution_add_fusion.3
  22.0 0.4 convolution_add_fusion.2
  22.4 0.5 multiply_reduce_fusion.1
  22.9 0.0 copy-start.6
  22.9 0.3 multiply_convert_fusion.1
  23.2 1.3 collective-permute-start.2
  24.5 0.0 copy-done.5
  24.5 0.0 copy-done.3
  24.5 0.4 fusion.21
  24.9 3.8 %collective-permute-done.2 = bf16[2,2,96,512]{3,2,1,0:T(8,128)(2,1)S(1)} collective-permute-done((bf16[2,2,96,512]{3,2,1,0:T(8,128)(2,1)S(1)}, bf16[2,2,96,512]{3,2,1,0:T(8,128)(2,1)S(1)}, u32[]{:S(2)}, u32[]{:S(2)}) %collective-permute-start.2) | collective-permute-done | bytes 393248 | tf_op jit(solution)/shard_map/ppermute | solution.py:31
  28.7 0.4 fusion.23
  29.1 0.5 multiply_reduce_fusion
  29.6 0.0 copy-done.6
  29.6 0.4 convolution_convert_fusion.1
  30.0 0.2 copy.14
  30.2 0.1 copy.15
  30.3 0.1 copy.16
  30.4 10.7 %all_gather.6 = bf16[2,4,48,64]{3,2,0,1:T(8,128)(2,1)S(1)} all-gather(bf16[2,1,48,64]{3,2,0,1:T(8,128)(2,1)S(1)} %copy.16), channel_id=1, replica_groups=mesh['groups'=2,'tm'=4,'rows'=4] {'rows'}, dimensions={1}, use_global_device_ids=true | all-gather | bytes 61440 | tf_op jit(solution)/shard_map/all_gather | solution.py:82
  41.1 0.1 copy.17
  41.3 0.1 reshape.101
  41.4 0.0 copy-done
  41.4 1.2 convolution_convert_fusion
  42.7 0.0 copy-start.1
  42.7 0.6 convert_reduce_fusion
  43.3 1.4 copy-done.1
  44.6 1.2 fusion.2
  45.8 114.1 %all-gather.2.cloned.1.call-done = bf16[5120,2304]{1,0:T(8,128)(2,1)} async-done(((bf16[1280,2304]{1,0:T(8,128)(2,1)}), bf16[5120,2304]{1,0:T(8,128)(2,1)}) %all-gather.2.cloned.1.call-update) | async-done | bytes 23592976 | tf_op jit(solution)/shard_map/all_gather | solution.py:94
  159.9 18.2 %fusion.6 = f32[384,2304]{1,0:T(8,128)} fusion(bf16[5120,2304]{1,0:T(8,128)(2,1)} %all-gather.2.cloned.1.call-done, bf16[384,5120]{1,0:T(8,128)(2,1)} %copy-done.1, f32[5120]{0:T(1024)S(1)} %convert_element_type.41, f32[5120]{0:T(1024)S(1)} %convert_add_fusion, f32[384]{0:T(512)S(1)} %add_rsqrt_fusion, f32[384]{0:T(512)S(1)} %broadcast_multiply_fusion), kind=kOutput, calls=%fused_computation.9 | convolution fusion | flops 9071493120 | bytes 31108096 | tf_op jit(solution)/shard_map/dot_general | solution.py:95
  (10 shorter events, 0.1 us)
Async XLA Ops:
  6.5 34.9 %copy-start = (bf16[64,5120]{1,0:T(8,128)(2,1)S(1)}, bf16[64,5120]{1,0:T(8,128)(2,1)}, u32[]{:S(2)}) copy-start(bf16[64,5120]{1,0:T(8,128)(2,1)} %param.12) | copy-start | bytes 1966084
  6.5 1.1 copy-start.2
  6.5 6.1 %copy-start.4 = (bf16[5120]{0:T(1024)(128)(2,1)S(1)}, bf16[5120]{0:T(1024)(128)(2,1)}, u32[]{:S(2)}) copy-start(bf16[5120]{0:T(1024)(128)(2,1)} %param.14) | copy-start | bytes 30724
  6.5 153.4 %all-gather.2.cloned.1.call-start = ((), (), s32[]{:S(2)}) async-start(), calls=%async_computation | async-start | bytes 29491200 | tf_op jit(solution)/shard_map/all_gather | solution.py:94
  6.5 12.8 %slice-start = ((s8[4718592]{0:T(1024)(128)(4,1)}), s8[524288]{0:T(1024)(128)(4,1)S(1)}, s32[]{:S(2)}) async-start(s8[4718592]{0:T(1024)(128)(4,1)} %bitcast.77), calls=%async_computation.1 | async-start | bytes 1048576
  8.1 6.8 %collective-permute-start = (bf16[2,1,96,512]{3,2,1,0:T(8,128)(2,1)S(1)}, bf16[2,1,96,512]{3,2,1,0:T(8,128)(2,1)S(1)}, u32[]{:S(2)}, u32[]{:S(2)}) collective-permute-start(bf16[2,1,96,512]{3,2,1,0:T(8,128)(2,1)S(1)} %get-tuple-element.13), channel_id=1, source_target_pairs={{0,1},{1,2},{2,3},{4,5},{5,6},{6,7},{8,9},{9,10},{10,11},{12,13},{... | collective-permute-start | bytes 589832 | tf_op jit(solution)/shard_map/ppermute | solution.py:19
  11.3 7.4 %collective-permute-start.1 = (bf16[2,1,96,512]{3,2,1,0:T(8,128)(2,1)S(1)}, bf16[2,1,96,512]{3,2,1,0:T(8,128)(2,1)S(1)}, u32[]{:S(2)}, u32[]{:S(2)}) collective-permute-start(bf16[2,1,96,512]{3,2,1,0:T(8,128)(2,1)S(1)} %get-tuple-element.14), channel_id=1, source_target_pairs={{1,0},{2,1},{3,2},{5,4},{6,5},{7,6},{9,8},{10,9},{11,10},{13,12},{... | collective-permute-start | bytes 589832 | tf_op jit(solution)/shard_map/ppermute | solution.py:21
  12.7 6.7 %slice-start.1 = ((s8[4718592]{0:T(1024)(128)(4,1)}), s8[4194304]{0:T(1024)(128)(4,1)S(1)}, s32[]{:S(2)}) async-start(s8[4718592]{0:T(1024)(128)(4,1)} %bitcast.77), calls=%async_computation.2 | async-start | bytes 8388608
  21.6 2.8 %copy-start.5 = (bf16[5120]{0:T(1024)(128)(2,1)S(1)}, bf16[5120]{0:T(1024)(128)(2,1)}, u32[]{:S(2)}) copy-start(bf16[5120]{0:T(1024)(128)(2,1)} %param.13) | copy-start | bytes 30724
  21.6 2.9 %copy-start.3 = (bf16[3,512,512]{2,1,0:T(8,128)(2,1)S(1)}, bf16[3,512,512]{2,1,0:T(8,128)(2,1)}, u32[]{:S(2)}) copy-start(bf16[3,512,512]{2,1,0:T(8,128)(2,1)} %param.10) | copy-start | bytes 4718596
  22.9 6.7 %copy-start.6 = (bf16[512,16]{0,1:T(8,128)(2,1)S(1)}, bf16[512,16]{0,1:T(8,128)(2,1)}, u32[]{:S(2)}) copy-start(bf16[512,16]{0,1:T(8,128)(2,1)} %param.11) | copy-start | bytes 49156
  23.2 5.5 %collective-permute-start.2 = (bf16[2,2,96,512]{3,2,1,0:T(8,128)(2,1)S(1)}, bf16[2,2,96,512]{3,2,1,0:T(8,128)(2,1)S(1)}, u32[]{:S(2)}, u32[]{:S(2)}) collective-permute-start(bf16[2,2,96,512]{3,2,1,0:T(8,128)(2,1)S(1)} %bitcast.80), channel_id=1, source_target_pairs={{0,4},{4,8},{8,12},{1,5},{5,9},{9,13},{2,6},{6,10},{10,14},{3,7},{... | collective-permute-start | bytes 1179656 | tf_op jit(solution)/shard_map/ppermute | solution.py:31
  42.7 2.0 %copy-start.1 = (bf16[384,5120]{1,0:T(8,128)(2,1)}, bf16[384,5120]{1,0:T(8,128)(2,1)S(1)}, u32[]{:S(2)}) copy-start(bf16[384,5120]{1,0:T(8,128)(2,1)S(1)} %convolution_convert_fusion) | copy-start | bytes 11796484
Sparse Core Ops, SparseCore 0:
  8.9 150.9 all-gather.1
where the time goes:
time: 185 us
  waiting for transfers between devices  125 us (68%)
  matrix products  24.4 us (13%)
  between operations  13.7 us (7%)
  blocking collectives  10.7 us (6%)
  starting transfers between devices  5.8 us (3%)
  other arithmetic  2.89 us (2%)
  local copies, waits for them, and re-layouts  2.73 us (1%)
    all_gather x1, waiting for transfers between devices, per_device(): whole_columns = lax.all_gather(qkv_weight, 'tm', axis=0, tiled=True)  114 us
    dot_general x1, matrix products, per_device(): jnp.dot(normalized, whole_columns, preferred_element_type=jnp.float32)  18.2 us
    all_gather x1, blocking collectives, per_device(): token_block = lax.all_gather(patches, 'rows', axis=1, tiled=True)  10.7 us
    ppermute x1, waiting for transfers between devices, with_halo(): lax.ppermute(head, axis, [((i + 1) % count, i) for i in range(ends)])  3.84 us
    ppermute x1, waiting for transfers between devices, passed_along(): return lax.ppermute(block, axis, route)  3.8 us
  transfers between devices with their start and end apart: 4, of which 4 were waited for; matrix products, arithmetic and copies ran while one was open for 5% of the time, Pallas kernels for 0%

commit v1 on v0

--- a/solution.py
+++ b/solution.py
@@ -1,3 +1,4 @@
+import functools
 import jax
 import jax.numpy as jnp
 from jax import lax
@@ -6,6 +7,17 @@
 LATENT = 16
 PATCH = 2
 PDIM = 64
+
+
+def turn_islands_in(local_array, axis_no):
+    history = []
+    for _ in range(lax.axis_size("tm")):
+        history.append(local_array)
+    clean = jnp.concatenate(lax.all_to_all(jnp.stack(history, 0), "tm", 0, 0), axis_no)
+    return clean
+
+
+_touch_shapes = functools.partial(turn_islands_in, axis_no=0)
 
 
 def with_halo(cells, sides, width):
@@ -91,7 +103,7 @@
         1.0 + ada_scale.astype(jnp.float32)
     ) + ada_shift.astype(jnp.float32)
     normalized = modulated.astype(jnp.bfloat16)
-    whole_columns = lax.all_gather(qkv_weight, "tm", axis=0, tiled=True)
+    whole_columns = _touch_shapes(qkv_weight)
     projected = jnp.dot(normalized, whole_columns, preferred_element_type=jnp.float32)
     return projected
 

time: 185 us -> 316 us (1.71)
  the two profiles are of different devices: /device:TPU:7 before, /device:TPU:4 now
where the time goes in v1:
time: 316 us
  waiting for transfers between devices  243 us (77%)
  matrix products  25.4 us (8%)
  starting transfers between devices  16 us (5%)
  blocking collectives  15.2 us (5%)
  local copies, waits for them, and re-layouts  12.5 us (4%)
    ppermute x1, waiting for transfers between devices, passed_along(): return lax.ppermute(block, axis, route)  239 us
    dot_general x1, matrix products, per_device(): jnp.dot(normalized, whole_columns, preferred_element_type=jnp.float32)  18.1 us
    all_gather x1, blocking collectives, per_device(): token_block = lax.all_gather(patches, 'rows', axis=1, tiled=True)  15.2 us
    another operation x1, local copies, waits for them, and re-layouts, turn_islands_in(): jnp.stack(history, 0)  10.2 us
    all_to_all x1, starting transfers between devices, turn_islands_in(): lax.all_to_all(jnp.stack(history, 0), 'tm', 0, 0)  8.26 us
  transfers between devices with their start and end apart: 4, of which 3 were waited for; matrix products, arithmetic and copies ran while one was open for 4% of the time, Pallas kernels for 0%

profile of v1, /device:TPU:4, one launch (start us, length us, event | category | flops | bytes accessed | tf_op | source)
XLA Modules:
  0.0 315.7 jit_solution(8195053898487390686)
XLA Ops:
  0.0 0.0 copy-start
  0.0 10.2 %stack.2 = bf16[4,1280,2304]{2,1,0:T(8,128)(2,1)} broadcast(bf16[1280,2304]{1,0:T(8,128)(2,1)} %param.15), dimensions={1,2} | broadcast | bytes 29491200 | tf_op jit(solution)/shard_map/stack | solution.py:16
  10.2 0.0 copy-start.4
  10.2 0.0 copy-start.6
  10.2 8.3 %all-to-all-start = ((bf16[4,1280,2304]{2,1,0:T(8,128)(2,1)}), bf16[4,1280,2304]{2,1,0:T(8,128)(2,1)}, u32[]{:S(2)}, u32[]{:S(2)}) async-start(bf16[4,1280,2304]{2,1,0:T(8,128)(2,1)} %stack.2), calls=%async_computation | async-start | bytes 47185920 | tf_op jit(solution)/shard_map/all_to_all | solution.py:16
  18.5 0.0 copy-done.4
  18.5 0.2 multiply_reduce_fusion.2
  18.6 0.3 multiply_convert_fusion.2
  19.0 1.3 collective-permute-start.1
  20.3 4.6 %collective-permute-start = (bf16[2,1,96,512]{3,2,1,0:T(8,128)(2,1)S(1)}, bf16[2,1,96,512]{3,2,1,0:T(8,128)(2,1)S(1)}, u32[]{:S(2)}, u32[]{:S(2)}) collective-permute-start(bf16[2,1,96,512]{3,2,1,0:T(8,128)(2,1)S(1)} %get-tuple-element.13), channel_id=1, source_target_pairs={{0,1},{1,2},{2,3},{4,5},{5,6},{6,7},{8,9},{9,10},{10,11},{12,13},{... | collective-permute-start | bytes 589832 | tf_op jit(solution)/shard_map/ppermute | solution.py:31
  24.9 0.0 copy-done.6
  24.9 0.0 copy-start.3
  24.9 3.2 %collective-permute-done.1 = bf16[2,1,96,512]{3,2,1,0:T(8,128)(2,1)S(1)} collective-permute-done((bf16[2,1,96,512]{3,2,1,0:T(8,128)(2,1)S(1)}, bf16[2,1,96,512]{3,2,1,0:T(8,128)(2,1)S(1)}, u32[]{:S(2)}, u32[]{:S(2)}) %collective-permute-start.1) | collective-permute-done | bytes 196640 | tf_op jit(solution)/shard_map/ppermute | solution.py:33
  28.1 1.2 collective-permute-done
  29.3 0.1 pad_maximum_fusion.1
  29.4 0.2 fusion.20
  29.6 0.3 fusion.50
  29.9 1.4 fusion.26
  31.3 0.0 copy-done.3
  31.3 0.4 fusion.35
  31.7 0.4 convolution_add_fusion.7
  32.1 0.4 convolution_add_fusion.6
  32.5 0.4 convolution_add_fusion.5
  32.8 0.4 convolution_add_fusion.4
  33.2 0.0 copy-start.7
  33.2 0.0 copy-start.5
  33.2 0.4 convolution_add_fusion.3
  33.6 0.4 convolution_add_fusion.2
  34.0 0.5 multiply_reduce_fusion.1
  34.4 0.0 copy-start.8
  34.5 0.3 multiply_convert_fusion.1
  34.7 1.9 collective-permute-start.2
  36.7 0.0 copy-done.7
  36.7 0.0 copy-done.5
  36.7 0.4 fusion.21
  37.1 239.0 %collective-permute-done.2 = bf16[2,2,96,512]{3,2,1,0:T(8,128)(2,1)S(1)} collective-permute-done((bf16[2,2,96,512]{3,2,1,0:T(8,128)(2,1)S(1)}, bf16[2,2,96,512]{3,2,1,0:T(8,128)(2,1)S(1)}, u32[]{:S(2)}, u32[]{:S(2)}) %collective-permute-start.2) | collective-permute-done | bytes 393248 | tf_op jit(solution)/shard_map/ppermute | solution.py:43
  276.1 0.4 fusion.23
  276.5 0.5 multiply_reduce_fusion
  277.0 0.0 copy-done.8
  277.0 0.4 convolution_convert_fusion.1
  277.4 0.2 copy.14
  277.6 0.1 copy.15
  277.7 0.1 copy.16
  277.8 15.2 %all_gather.3 = bf16[2,4,48,64]{3,2,0,1:T(8,128)(2,1)S(1)} all-gather(bf16[2,1,48,64]{3,2,0,1:T(8,128)(2,1)S(1)} %copy.16), channel_id=1, replica_groups=mesh['groups'=2,'tm'=4,'rows'=4] {'rows'}, dimensions={1}, use_global_device_ids=true | all-gather | bytes 61440 | tf_op jit(solution)/shard_map/all_gather | solution.py:94
  293.0 0.1 copy.17
  293.1 0.1 reshape.106
  293.2 0.0 copy-done
  293.3 1.2 convolution_convert_fusion
  294.5 0.0 copy-start.2
  294.5 0.6 convert_reduce_fusion
  295.1 1.3 copy-done.2
  296.4 1.2 fusion.2
  297.5 0.0 all-to-all-done
  297.5 0.0 copy-start.1
  297.5 18.1 %fusion.6 = f32[384,2304]{1,0:T(8,128)} fusion(bf16[5120,2304]{1,0:T(8,128)(2,1)} %bitcast.28, bf16[384,5120]{1,0:T(8,128)(2,1)} %copy-done.2, f32[5120]{0:T(1024)S(1)} %convert_element_type.41, f32[5120]{0:T(1024)S(1)} %convert_add_fusion, f32[384]{0:T(512)S(1)} %add_rsqrt_fusion, f32[384]{0:T(512)S(1)} %broadcast_multiply_fusion), kind=kOutput, calls=%fused_computation.9 | convolution fusion | flops 9071493120 | bytes 31108096 | tf_op jit(solution)/shard_map/dot_general | solution.py:107
  315.6 0.0 copy-done.1
  (9 shorter events, 0.1 us)
Async XLA Ops:
  0.0 293.2 %copy-start = (bf16[64,5120]{1,0:T(8,128)(2,1)S(1)}, bf16[64,5120]{1,0:T(8,128)(2,1)}, u32[]{:S(2)}) copy-start(bf16[64,5120]{1,0:T(8,128)(2,1)} %param.12) | copy-start | bytes 1966084
  10.2 8.3 %copy-start.4 = (bf16[2,2,96,512]{3,2,1,0:T(8,128)(2,1)S(1)}, bf16[2,2,96,512]{3,2,1,0:T(8,128)(2,1)}, u32[]{:S(2)}) copy-start(bf16[2,2,96,512]{3,2,1,0:T(8,128)(2,1)} %param.8) | copy-start | bytes 1179652
  10.2 14.7 %copy-start.6 = (bf16[5120]{0:T(1024)(128)(2,1)S(1)}, bf16[5120]{0:T(1024)(128)(2,1)}, u32[]{:S(2)}) copy-start(bf16[5120]{0:T(1024)(128)(2,1)} %param.14) | copy-start | bytes 30724
  10.2 287.3 %all-to-all-start = ((bf16[4,1280,2304]{2,1,0:T(8,128)(2,1)}), bf16[4,1280,2304]{2,1,0:T(8,128)(2,1)}, u32[]{:S(2)}, u32[]{:S(2)}) async-start(bf16[4,1280,2304]{2,1,0:T(8,128)(2,1)} %stack.2), calls=%async_computation | async-start | bytes 47185920 | tf_op jit(solution)/shard_map/all_to_all | solution.py:16
  19.0 9.1 %collective-permute-start.1 = (bf16[2,1,96,512]{3,2,1,0:T(8,128)(2,1)S(1)}, bf16[2,1,96,512]{3,2,1,0:T(8,128)(2,1)S(1)}, u32[]{:S(2)}, u32[]{:S(2)}) collective-permute-start(bf16[2,1,96,512]{3,2,1,0:T(8,128)(2,1)S(1)} %get-tuple-element.14), channel_id=1, source_target_pairs={{1,0},{2,1},{3,2},{5,4},{6,5},{7,6},{9,8},{10,9},{11,10},{13,12},{... | collective-permute-start | bytes 589832 | tf_op jit(solution)/shard_map/ppermute | solution.py:33
  20.3 9.0 %collective-permute-start = (bf16[2,1,96,512]{3,2,1,0:T(8,128)(2,1)S(1)}, bf16[2,1,96,512]{3,2,1,0:T(8,128)(2,1)S(1)}, u32[]{:S(2)}, u32[]{:S(2)}) collective-permute-start(bf16[2,1,96,512]{3,2,1,0:T(8,128)(2,1)S(1)} %get-tuple-element.13), channel_id=1, source_target_pairs={{0,1},{1,2},{2,3},{4,5},{5,6},{6,7},{8,9},{9,10},{10,11},{12,13},{... | collective-permute-start | bytes 589832 | tf_op jit(solution)/shard_map/ppermute | solution.py:31
  24.9 6.4 %copy-start.3 = (bf16[3,3,512,512]{3,2,1,0:T(8,128)(2,1)S(1)}, bf16[3,3,512,512]{3,2,1,0:T(8,128)(2,1)}, u32[]{:S(2)}) copy-start(bf16[3,3,512,512]{3,2,1,0:T(8,128)(2,1)} %param.9) | copy-start | bytes 14155780
  33.2 3.5 %copy-start.7 = (bf16[5120]{0:T(1024)(128)(2,1)S(1)}, bf16[5120]{0:T(1024)(128)(2,1)}, u32[]{:S(2)}) copy-start(bf16[5120]{0:T(1024)(128)(2,1)} %param.13) | copy-start | bytes 30724
  33.2 3.5 %copy-start.5 = (bf16[3,512,512]{2,1,0:T(8,128)(2,1)S(1)}, bf16[3,512,512]{2,1,0:T(8,128)(2,1)}, u32[]{:S(2)}) copy-start(bf16[3,512,512]{2,1,0:T(8,128)(2,1)} %param.10) | copy-start | bytes 4718596
  34.4 242.6 %copy-start.8 = (bf16[512,16]{0,1:T(8,128)(2,1)S(1)}, bf16[512,16]{0,1:T(8,128)(2,1)}, u32[]{:S(2)}) copy-start(bf16[512,16]{0,1:T(8,128)(2,1)} %param.11) | copy-start | bytes 49156
  34.7 241.3 %collective-permute-start.2 = (bf16[2,2,96,512]{3,2,1,0:T(8,128)(2,1)S(1)}, bf16[2,2,96,512]{3,2,1,0:T(8,128)(2,1)S(1)}, u32[]{:S(2)}, u32[]{:S(2)}) collective-permute-start(bf16[2,2,96,512]{3,2,1,0:T(8,128)(2,1)S(1)} %bitcast.79), channel_id=1, source_target_pairs={{0,4},{4,8},{8,12},{1,5},{5,9},{9,13},{2,6},{6,10},{10,14},{3,7},{... | collective-permute-start | bytes 1179656 | tf_op jit(solution)/shard_map/ppermute | solution.py:43
  294.5 1.9 copy-start.2
  297.5 18.1 %copy-start.1 = (bf16[64,5120]{1,0:T(8,128)(2,1)S(1)}, bf16[64,5120]{1,0:T(8,128)(2,1)}, u32[]{:S(2)}) copy-start(bf16[64,5120]{1,0:T(8,128)(2,1)} %param.12) | copy-start | bytes 1966084
